TPU v7x, 256 devices: a whole 4x4x8 slice. The times are simulated.
256 devices in a mesh: row: 32 (over y, z), col: 8 (over x, core).
Axes of the slice: x: 4, y: 4, z: 8, core: 2. Of those that a mesh axis runs over, the one named last changes fastest.
Arguments:
- sim_window: bfloat16 [6144, 6144], P('row', 'col'), as said below
- sim_rest: bfloat16 [6144, 113856], P('row', 'col'), may hold values from -6 to 6
- joined_partner_pairs: int32 [768, 2], replicated, may hold values from 0 to 6143, as said below
- cluster_member_count: int32 [6144], replicated, may hold values from 1 to 64
Outputs:
- window_out: bfloat16 [6144, 6144], P('row', 'col')
- rest_out: bfloat16 [6144, 113856], P('row', 'col')
Inputs may be any that keep to these rules, and one draw needn't show every extreme that they name: `joined_partner_pairs`: each row is (survivor, partner); no window item appears twice in the whole list. Each aligned block of 192 items holds exactly 24 partners. For any two aligned blocks (possibly the same), at most 3 pairs have their partner in the first and their survivor in the second, and some two blocks have exactly 3. Nearly symmetric: sim_window[i, j] is close to sim_window[j, i].
All inputs are finite; a program needn't handle non-finite values.
Results may differ from a plain program's by a relative error of at most 0.001.
Values may be sent and summed in bfloat16 or wider, within the bound.
No kernel may reach another device: no remote copies, remote signals or barrier semaphores. Data moves between devices by JAX's collectives and lax.ppermute only.
A program may use at most 128 MiB of HBM per device.

v0:
```python
import jax
import jax.numpy as jnp
from jax import lax
from jax.sharding import PartitionSpec as P


def pairing_tables(joined_partner_pairs, cluster_member_count):
    lasting_node = joined_partner_pairs[:, 0]
    vanishing_node = joined_partner_pairs[:, 1]
    remaining_size = cluster_member_count[lasting_node].astype(jnp.float32)
    absorbed_size = cluster_member_count[vanishing_node].astype(jnp.float32)
    joined_cluster_size = remaining_size + absorbed_size
    return (
        lasting_node,
        vanishing_node,
        remaining_size / joined_cluster_size,
        absorbed_size / joined_cluster_size,
    )


def item_weight_values(node_labels, lasting_node, vanishing_node, retained_pair, selected_pair):
    lasting_mask = node_labels[:, None] == lasting_node[None, :]
    belongs_mask = node_labels[:, None] == vanishing_node[None, :]
    lasting_real_mask = lasting_mask.astype(jnp.float32)
    matched_mask = jnp.sum((lasting_mask | belongs_mask).astype(jnp.float32), axis=1)
    retained_entries = (
        1.0 - matched_mask + jnp.sum(lasting_real_mask * retained_pair[None, :], axis=1)
    )
    selected_entries = jnp.sum(lasting_real_mask * selected_pair[None, :], axis=1)
    donor_position = jnp.sum(jnp.where(lasting_mask, vanishing_node[None, :], 0), axis=1)
    return (retained_entries, selected_entries, donor_position)


def shards(sim_window, sim_rest, joined_partner_pairs, cluster_member_count):
    row_number_total = sim_window.shape[0]
    col_count = sim_window.shape[1]
    blocks = lax.axis_size("row")
    local_block = lax.axis_index("row")
    my_col = lax.axis_index("col")
    lasting_node, vanishing_node, retained_pair, selected_pair = pairing_tables(
        joined_partner_pairs, cluster_member_count
    )
    row_sequence = jnp.arange(row_number_total, dtype=jnp.int32)
    retained_entries, selected_entries, ignored = item_weight_values(
        local_block * row_number_total + row_sequence,
        lasting_node,
        vanishing_node,
        retained_pair,
        selected_pair,
    )
    src_block = vanishing_node // row_number_total
    destination_block = lasting_node // row_number_total
    pair_count = joined_partner_pairs.shape[0]
    pair_order = jnp.arange(pair_count, dtype=jnp.int32)
    earlier = pair_order[None, :] < pair_order[:, None]
    slot_width = row_number_total // 8
    same_route = src_block[None, :] == src_block[:, None]
    slot_rank = jnp.sum((earlier & same_route).astype(jnp.int32), axis=1)
    recv_slot = src_block * slot_width + slot_rank
    recv_width = blocks * slot_width
    mine_src = src_block == local_block
    slot_hot = (
        (jnp.arange(slot_width, dtype=jnp.int32)[:, None] == slot_rank[None, :]) & mine_src[None, :]
    ).astype(jnp.bfloat16)
    row_hot = (
        (vanishing_node - local_block * row_number_total)[:, None] == row_sequence[None, :]
    ).astype(jnp.bfloat16)
    selector = jnp.dot(slot_hot, row_hot, preferred_element_type=jnp.float32).astype(jnp.bfloat16)
    send_window = jnp.dot(selector, sim_window, preferred_element_type=jnp.float32).astype(
        jnp.bfloat16
    )
    send_rest = jnp.dot(selector, sim_rest, preferred_element_type=jnp.float32).astype(jnp.bfloat16)
    local_destination = destination_block == local_block
    target_hot = (
        ((lasting_node - local_block * row_number_total)[None, :] == row_sequence[:, None])
        & local_destination[None, :]
    ).astype(jnp.bfloat16)
    recv_hot = (recv_slot[:, None] == jnp.arange(recv_width, dtype=jnp.int32)[None, :]).astype(
        jnp.bfloat16
    )
    placement = jnp.dot(target_hot, recv_hot, preferred_element_type=jnp.float32).astype(
        jnp.bfloat16
    )
    placed_window = jnp.dot(
        placement,
        lax.all_gather(send_window, "row", axis=0, tiled=True),
        preferred_element_type=jnp.float32,
    )
    placed_rest = jnp.dot(
        placement,
        lax.all_gather(send_rest, "row", axis=0, tiled=True),
        preferred_element_type=jnp.float32,
    )
    mixed_window = (
        retained_entries[:, None] * sim_window.astype(jnp.float32)
        + selected_entries[:, None] * placed_window
    ).astype(jnp.bfloat16)
    rest_out = (
        retained_entries[:, None] * sim_rest.astype(jnp.float32)
        + selected_entries[:, None] * placed_rest
    ).astype(jnp.bfloat16)
    col_iota = jnp.arange(col_count, dtype=jnp.int32)
    column_identifiers = my_col * col_count + col_iota
    column_retained, column_selected, column_provider = item_weight_values(
        column_identifiers, lasting_node, vanishing_node, retained_pair, selected_pair
    )
    piece = lax.all_gather(mixed_window, "col", axis=1, tiled=True)
    piece_width = piece.shape[1]
    picker = (jnp.arange(piece_width, dtype=jnp.int32)[:, None] == column_provider[None, :]).astype(
        jnp.bfloat16
    )
    gathered = jnp.dot(piece, picker, preferred_element_type=jnp.float32)
    window_out = (
        column_retained[None, :] * mixed_window.astype(jnp.float32)
        + column_selected[None, :] * gathered
    ).astype(jnp.bfloat16)
    return (window_out, rest_out)


def solution(mesh):
    in_specs = (P("row", "col"), P("row", "col"), P(), P())
    out_specs = (P("row", "col"), P("row", "col"))
    return jax.shard_map(shards, mesh=mesh, in_specs=in_specs, out_specs=out_specs, check_vma=False)
```

profile of v0, /device:TPU:1, one launch (start us, length us, event | category | flops | bytes accessed | tf_op | source)
XLA Modules:
  0.0 313.5 jit_solution(18282270828736118344)
XLA Ops:
  7.2 0.0 copy-start
  7.2 0.0 all-gather.4.cloned.1.call-start
  7.2 0.8 fusion.32
  8.1 0.4 convert_reduce_fusion
  8.5 0.3 convolution_convert_fusion.2
  8.7 1.8 convolution_convert_fusion.1
  10.5 0.0 all-gather.4.cloned.1.call-update
  10.6 0.0 all-gather.6.cloned.1.call-start
  10.6 0.0 copy-done
  10.6 4.5 %gather_fusion = s32[768]{0:T(1024)S(1)} fusion(s32[6144]{0:T(1024)S(1)} %copy-done, s32[1024]{0:T(1024)S(1)} %get-tuple-element.25), kind=kCustom, calls=%fused_computation | custom fusion | bytes 9216 | tf_op jit(solution)/shard_map/gather | solution.py:10
  15.1 0.0 copy-start.2
  15.1 4.5 %gather_fusion.1 = s32[768]{0:T(1024)S(1)} fusion(s32[6144]{0:T(1024)S(1)} %copy-done, s32[1024]{0:T(1024)S(1)} %get-tuple-element.24), kind=kCustom, calls=%fused_computation.1 | custom fusion | bytes 9216 | tf_op jit(solution)/shard_map/gather | solution.py:11
  19.6 0.3 convert_reduce_fusion.2
  20.0 0.8 fusion.14
  20.8 65.7 %all-gather.4.cloned.1.call-done = bf16[768,768]{1,0:T(8,128)(2,1)} async-done(((bf16[24,768]{1,0:T(8,128)(2,1)}), bf16[768,768]{1,0:T(8,128)(2,1)}) %all-gather.4.cloned.1.call-update) | async-done | bytes 1179664 | tf_op jit(solution)/shard_map/all_gather | solution.py:86
  86.5 0.0 copy-done.2
  86.5 2.4 fusion.13
  88.9 0.0 all-gather.6.cloned.1.call-update
  88.9 0.0 copy-start.1
  88.9 0.2 all-gather.8.cloned.1.call-start
  89.1 4.3 %convolution_convert_fusion = bf16[24,14232]{1,0:T(8,128)(2,1)} fusion(bf16[24,192]{1,0:T(8,128)(2,1)S(1)} %convolution_convert_fusion.2, bf16[192,14232]{1,0:T(8,128)(2,1)} %param.5), kind=kOutput, calls=%fused_computation.7 | convolution fusion | flops 131503680 | bytes 6157440 | tf_op jit(solution)/shard_map/dot_general | solution.py:72
  93.4 0.0 all-gather.8.cloned.1.call-update
  93.4 0.4 fusion.6
  93.8 0.9 convert_reduce_fusion.1
  94.7 25.4 %all-gather.6.cloned.1.call-done = bf16[192,6144]{1,0:T(8,128)(2,1)} async-done(((bf16[192,768]{1,0:T(8,128)(2,1)}), bf16[192,6144]{1,0:T(8,128)(2,1)}) %all-gather.6.cloned.1.call-update) | async-done | bytes 2359312 | tf_op jit(solution)/shard_map/all_gather | solution.py:107
  120.1 0.0 copy-done.1
  120.1 6.4 %fusion.12 = bf16[192,768]{1,0:T(8,128)(2,1)} fusion(bf16[192,6144]{1,0:T(8,128)(2,1)} %all-gather.6.cloned.1.call-done, s32[768]{0:T(1024)S(1)} %fusion.6, bf16[192,768]{1,0:T(8,128)(2,1)S(1)} %copy-done.1, f32[768]{0:T(1024)S(1)} %get-tuple-element.3, f32[768]{0:T(1024)S(1)} %subtract_add_fusion), kind=kOutput, calls=%fused_computation.26 | convolution fusion | flops 1817395200 | bytes 2958336 | tf_op jit(solution)/shard_map/dot_general | solution.py:112
  126.5 162.6 %all-gather.8.cloned.1.call-done = bf16[768,14232]{1,0:T(8,128)(2,1)} async-done(((bf16[24,14232]{1,0:T(8,128)(2,1)}), bf16[768,14232]{1,0:T(8,128)(2,1)}) %all-gather.8.cloned.1.call-update) | async-done | bytes 21860368 | tf_op jit(solution)/shard_map/all_gather | solution.py:91
  289.1 17.9 %fusion.2 = bf16[192,14232]{1,0:T(8,128)(2,1)} fusion(bf16[192,768]{1,0:T(8,128)(2,1)S(1)} %fusion.14, bf16[768,14232]{1,0:T(8,128)(2,1)} %all-gather.8.cloned.1.call-done, bf16[192,14232]{1,0:T(8,128)(2,1)} %param.5, f32[192]{0:T(256)S(1)} %get-tuple-element.12, f32[192]{0:T(256)S(1)} %subtract_add_fusion.1), kind=kOutput, calls=%fused_computation.6 | convolution fusion | flops 4210850304 | bytes 33086976 | tf_op jit(solution)/shard_map/dot_general | solution.py:89
  (10 shorter events, 0.1 us)
Async XLA Ops:
  7.2 3.5 %copy-start = (s32[6144]{0:T(1024)S(1)}, s32[6144]{0:T(1024)}, u32[]{:S(2)}) copy-start(s32[6144]{0:T(1024)} %param.7) | copy-start | bytes 73732
  7.2 79.3 %all-gather.4.cloned.1.call-start = ((), (), s32[]{:S(2)}) async-start(), calls=%async_computation | async-start | bytes 1216512 | tf_op jit(solution)/shard_map/all_gather | solution.py:86
  10.6 109.6 %all-gather.6.cloned.1.call-start = ((), (), s32[]{:S(2)}) async-start(), calls=%async_computation.1 | async-start | bytes 2654208 | tf_op jit(solution)/shard_map/all_gather | solution.py:107
  15.1 71.4 %copy-start.2 = (bf16[192,768]{1,0:T(8,128)(2,1)S(1)}, bf16[192,768]{1,0:T(8,128)(2,1)}, u32[]{:S(2)}) copy-start(bf16[192,768]{1,0:T(8,128)(2,1)} %param.4) | copy-start | bytes 884740
  88.9 31.2 %copy-start.1 = (bf16[192,768]{1,0:T(8,128)(2,1)S(1)}, bf16[192,768]{1,0:T(8,128)(2,1)}, u32[]{:S(2)}) copy-start(bf16[192,768]{1,0:T(8,128)(2,1)} %fusion.13) | copy-start | bytes 884740
  88.9 200.2 %all-gather.8.cloned.1.call-start = ((), (), s32[]{:S(2)}) async-start(), calls=%async_computation.2 | async-start | bytes 22708224 | tf_op jit(solution)/shard_map/all_gather | solution.py:91
Sparse Core Ops, SparseCore 0:
  11.1 75.2 all-gather.3
  89.0 31.0 all-gather.5
  123.3 165.8 all-gather.7
where the time goes:
time: 314 us
  waiting for transfers between devices  254 us (81%)
  matrix products  33.7 us (11%)
  between operations  13.9 us (4%)
  local copies, waits for them, and re-layouts  8.95 us (3%)
    all_gather x1, waiting for transfers between devices, shards(): lax.all_gather(send_rest, 'row', axis=0, tiled=True)  163 us
    all_gather x1, waiting for transfers between devices, shards(): lax.all_gather(send_window, 'row', axis=0, tiled=True)  65.7 us
    all_gather x1, waiting for transfers between devices, shards(): piece = lax.all_gather(mixed_window, 'col', axis=1, tiled=True)  25.4 us
    dot_general x1, matrix products, shards(): jnp.dot(placement, lax.all_gather(send_rest, 'row', axis=0, tiled=True),...  17.9 us
    dot_general x1, matrix products, shards(): gathered = jnp.dot(piece, picker, preferred_element_type=jnp.float32)  6.39 us
  transfers between devices with their start and end apart: 3, of which 3 were waited for; matrix products, arithmetic and copies ran while one was open for 7% of the time, Pallas kernels for 0%

commit v1 on v0

--- a/solution.py
+++ b/solution.py
@@ -81,10 +81,12 @@
     placement = jnp.dot(target_hot, recv_hot, preferred_element_type=jnp.float32).astype(
         jnp.bfloat16
     )
+    resolve_the_columns = lambda shard_in: jnp.concatenate(
+        lax.all_to_all(jnp.stack([shard_in for _ in range(lax.axis_size("row"))]), "row", 0, 0),
+        axis=0,
+    )
     placed_window = jnp.dot(
-        placement,
-        lax.all_gather(send_window, "row", axis=0, tiled=True),
-        preferred_element_type=jnp.float32,
+        placement, resolve_the_columns(send_window), preferred_element_type=jnp.float32
     )
     placed_rest = jnp.dot(
         placement,

time: 314 us -> 275 us (0.88)
  waiting for transfers between devices: 254 us -> 204 us
  starting transfers between devices: 0.3 us -> 12.3 us
    all_gather x1 -> x0, waiting for transfers between devices: 65.7 us -> none  [shards(): lax.all_gather(send_window, 'row', axis=0, tiled=True)]
    all_to_all x0 -> x1, waiting for transfers between devices: none -> 17.3 us  [shards(): lax.all_to_all(jnp.stack([shard_in for _ in range(lax.axis_size('row'))])...]
    all_to_all x0 -> x1, starting transfers between devices: none -> 12 us  [shards(): lax.all_to_all(jnp.stack([shard_in for _ in range(lax.axis_size('row'))])...]
  transfers between devices with their start and end apart: 3 -> 3, of which waited for: 3 -> 3; matrix products, arithmetic and copies ran while one was open for 7% -> 8% of each run, Pallas kernels for 0% -> 0%
where the time goes in v1:
time: 275 us
  waiting for transfers between devices  204 us (74%)
  matrix products  31.8 us (12%)
  between operations  14.2 us (5%)
  starting transfers between devices  12.3 us (4%)
  local copies, waits for them, and re-layouts  10 us (4%)
  other arithmetic  2.91 us (1%)
    all_gather x1, waiting for transfers between devices, shards(): lax.all_gather(send_rest, 'row', axis=0, tiled=True)  163 us
    all_gather x1, waiting for transfers between devices, shards(): piece = lax.all_gather(mixed_window, 'col', axis=1, tiled=True)  23.6 us
    dot_general x1, matrix products, shards(): jnp.dot(placement, lax.all_gather(send_rest, 'row', axis=0, tiled=True),...  17.9 us
    all_to_all x1, waiting for transfers between devices, shards(): lax.all_to_all(jnp.stack([shard_in for _ in range(lax.axis_size('row'))])...  17.3 us
    all_to_all x1, starting transfers between devices, shards(): lax.all_to_all(jnp.stack([shard_in for _ in range(lax.axis_size('row'))])...  12 us
    dot_general x1, matrix products, shards(): gathered = jnp.dot(piece, picker, preferred_element_type=jnp.float32)  6.39 us
  transfers between devices with their start and end apart: 3, of which 3 were waited for; matrix products, arithmetic and copies ran while one was open for 8% of the time, Pallas kernels for 0%

profile of v1, /device:TPU:1, one launch (start us, length us, event | category | flops | bytes accessed | tf_op | source)
XLA Modules:
  0.0 274.8 jit_solution(7704345066781727186)
XLA Ops:
  7.2 0.0 copy-start
  7.2 0.8 fusion.32
  8.0 0.4 convert_reduce_fusion
  8.4 0.3 convolution_convert_fusion.2
  8.7 1.2 convolution_convert_fusion.1
  9.9 1.1 stack.2
  11.0 12.0 %all-to-all-start = ((bf16[32,24,768]{2,1,0:T(8,128)(2,1)}), bf16[32,24,768]{2,1,0:T(8,128)(2,1)S(1)}, u32[]{:S(2)}, u32[]{:S(2)}) async-start(bf16[32,24,768]{2,1,0:T(8,128)(2,1)} %stack.2), calls=%async_computation | async-start | bytes 2359296 | tf_op jit(solution)/shard_map/all_to_all | solution.py:85
  23.0 0.0 all-gather.3.cloned.1.call-start
  23.1 0.0 copy-done
  23.1 4.5 %gather_fusion = s32[768]{0:T(1024)S(1)} fusion(s32[6144]{0:T(1024)S(1)} %copy-done, s32[1024]{0:T(1024)S(1)} %get-tuple-element.25), kind=kCustom, calls=%fused_computation | custom fusion | bytes 9216 | tf_op jit(solution)/shard_map/gather | solution.py:10
  27.5 0.0 copy-start.2
  27.5 4.5 %gather_fusion.1 = s32[768]{0:T(1024)S(1)} fusion(s32[6144]{0:T(1024)S(1)} %copy-done, s32[1024]{0:T(1024)S(1)} %get-tuple-element.24), kind=kCustom, calls=%fused_computation.1 | custom fusion | bytes 9216 | tf_op jit(solution)/shard_map/gather | solution.py:11
  32.1 0.3 convert_reduce_fusion.2
  32.4 0.8 fusion.14
  33.2 17.3 %all-to-all-done = bf16[32,24,768]{2,1,0:T(8,128)(2,1)S(1)} async-done(((bf16[32,24,768]{2,1,0:T(8,128)(2,1)}), bf16[32,24,768]{2,1,0:T(8,128)(2,1)S(1)}, u32[]{:S(2)}, u32[]{:S(2)}) %all-to-all-start) | async-done | bytes 1179680 | tf_op jit(solution)/shard_map/all_to_all | solution.py:85
  50.5 0.0 copy-done.2
  50.5 1.1 fusion.13
  51.7 0.0 all-gather.3.cloned.1.call-update
  51.7 0.0 copy-start.1
  51.7 0.2 all-gather.5.cloned.1.call-start
  51.9 4.3 %convolution_convert_fusion = bf16[24,14232]{1,0:T(8,128)(2,1)} fusion(bf16[24,192]{1,0:T(8,128)(2,1)S(1)} %convolution_convert_fusion.2, bf16[192,14232]{1,0:T(8,128)(2,1)} %param.5), kind=kOutput, calls=%fused_computation.7 | convolution fusion | flops 131503680 | bytes 6157440 | tf_op jit(solution)/shard_map/dot_general | solution.py:72
  56.2 0.0 all-gather.5.cloned.1.call-update
  56.2 0.4 fusion.6
  56.6 0.9 convert_reduce_fusion.1
  57.5 23.6 %all-gather.3.cloned.1.call-done = bf16[192,6144]{1,0:T(8,128)(2,1)} async-done(((bf16[192,768]{1,0:T(8,128)(2,1)}), bf16[192,6144]{1,0:T(8,128)(2,1)}) %all-gather.3.cloned.1.call-update) | async-done | bytes 2359312 | tf_op jit(solution)/shard_map/all_gather | solution.py:109
  81.1 0.0 copy-done.1
  81.1 6.4 %fusion.12 = bf16[192,768]{1,0:T(8,128)(2,1)} fusion(bf16[192,6144]{1,0:T(8,128)(2,1)} %all-gather.3.cloned.1.call-done, s32[768]{0:T(1024)S(1)} %fusion.6, bf16[192,768]{1,0:T(8,128)(2,1)S(1)} %copy-done.1, f32[768]{0:T(1024)S(1)} %get-tuple-element.3, f32[768]{0:T(1024)S(1)} %subtract_add_fusion), kind=kOutput, calls=%fused_computation.26 | convolution fusion | flops 1817395200 | bytes 2958336 | tf_op jit(solution)/shard_map/dot_general | solution.py:114
  87.5 162.6 %all-gather.5.cloned.1.call-done = bf16[768,14232]{1,0:T(8,128)(2,1)} async-done(((bf16[24,14232]{1,0:T(8,128)(2,1)}), bf16[768,14232]{1,0:T(8,128)(2,1)}) %all-gather.5.cloned.1.call-update) | async-done | bytes 21860368 | tf_op jit(solution)/shard_map/all_gather | solution.py:93
  250.1 17.9 %fusion.2 = bf16[192,14232]{1,0:T(8,128)(2,1)} fusion(bf16[192,768]{1,0:T(8,128)(2,1)S(1)} %fusion.14, bf16[768,14232]{1,0:T(8,128)(2,1)} %all-gather.5.cloned.1.call-done, bf16[192,14232]{1,0:T(8,128)(2,1)} %param.5, f32[192]{0:T(256)S(1)} %get-tuple-element.12, f32[192]{0:T(256)S(1)} %subtract_add_fusion.1), kind=kOutput, calls=%fused_computation.6 | convolution fusion | flops 4210850304 | bytes 33086976 | tf_op jit(solution)/shard_map/dot_general | solution.py:91
  (10 shorter events, 0.1 us)
Async XLA Ops:
  7.2 15.9 %copy-start = (s32[6144]{0:T(1024)S(1)}, s32[6144]{0:T(1024)}, u32[]{:S(2)}) copy-start(s32[6144]{0:T(1024)} %param.7) | copy-start | bytes 73732
  11.0 39.6 %all-to-all-start = ((bf16[32,24,768]{2,1,0:T(8,128)(2,1)}), bf16[32,24,768]{2,1,0:T(8,128)(2,1)S(1)}, u32[]{:S(2)}, u32[]{:S(2)}) async-start(bf16[32,24,768]{2,1,0:T(8,128)(2,1)} %stack.2), calls=%async_computation | async-start | bytes 2359296 | tf_op jit(solution)/shard_map/all_to_all | solution.py:85
  23.0 58.1 %all-gather.3.cloned.1.call-start = ((), (), s32[]{:S(2)}) async-start(), calls=%async_computation.1 | async-start | bytes 2654208 | tf_op jit(solution)/shard_map/all_gather | solution.py:109
  27.5 23.0 %copy-start.2 = (bf16[192,768]{1,0:T(8,128)(2,1)S(1)}, bf16[192,768]{1,0:T(8,128)(2,1)}, u32[]{:S(2)}) copy-start(bf16[192,768]{1,0:T(8,128)(2,1)} %param.4) | copy-start | bytes 884740
  51.7 29.4 %copy-start.1 = (bf16[192,768]{1,0:T(8,128)(2,1)S(1)}, bf16[192,768]{1,0:T(8,128)(2,1)}, u32[]{:S(2)}) copy-start(bf16[192,768]{1,0:T(8,128)(2,1)} %fusion.13) | copy-start | bytes 884740
  51.7 198.4 %all-gather.5.cloned.1.call-start = ((), (), s32[]{:S(2)}) async-start(), calls=%async_computation.2 | async-start | bytes 22708224 | tf_op jit(solution)/shard_map/all_gather | solution.py:93
Sparse Core Ops, SparseCore 0:
  51.8 29.2 all-gather.2
  84.2 165.8 all-gather.4
